TPU v7x, 32 devices: a whole 2x2x4 slice. The times are simulated.
32 devices in a mesh: fsdp: 8 (over z, y), tp: 4 (over x, core).
Axes of the slice: x: 2, y: 2, z: 4, core: 2. Of those that a mesh axis runs over, the one named last changes fastest.
Arguments:
- layer_input: bfloat16 [2, 8192, 768], P(None, ('fsdp', 'tp')), may hold values from -6 to 6
- out_grad: bfloat16 [2, 8192, 768], P(None, ('fsdp', 'tp')), may hold values from -6 to 6
- ln1_gain: float32 [768], replicated, may hold values from 0.5 to 1.5
- ln1_bias: float32 [768], replicated, may hold values from -3 to 3
- w_query: bfloat16 [768, 768], P('fsdp', 'tp'), may hold values from -0.21875 to 0.21875
- w_key: bfloat16 [768, 768], P('fsdp', 'tp'), may hold values from -0.21875 to 0.21875
- w_value: bfloat16 [768, 768], P('fsdp', 'tp'), may hold values from -0.21875 to 0.21875
- conv_query: float32 [3, 768], replicated, may hold values from -3 to 3
- conv_key: float32 [3, 768], replicated, may hold values from -3 to 3
- conv_value: float32 [3, 768], replicated, may hold values from -3 to 3
- w_out: bfloat16 [768, 768], P('tp', 'fsdp'), may hold values from -1.25 to 1.25
- ln2_gain: float32 [768], replicated, may hold values from 0.5 to 1.5
- ln2_bias: float32 [768], replicated, may hold values from -3 to 3
- w_up: bfloat16 [768, 3072], P('fsdp', 'tp'), may hold values from -0.21875 to 0.21875
- up_bias: float32 [3072], replicated, may hold values from -3 to 3
- w_down: bfloat16 [3072, 768], P('tp', 'fsdp'), may hold values from -0.109375 to 0.109375
- down_bias: float32 [768], replicated, may hold values from -3 to 3
Outputs:
- layer_out: bfloat16 [2, 8192, 768], P(None, ('fsdp', 'tp'))
- in_grad: bfloat16 [2, 8192, 768], P(None, ('fsdp', 'tp'))
- ln1_gain_grad: float32 [768], replicated
- ln1_bias_grad: float32 [768], replicated
- w_query_grad: float32 [768, 768], P('fsdp', 'tp')
- w_key_grad: float32 [768, 768], P('fsdp', 'tp')
- w_value_grad: float32 [768, 768], P('fsdp', 'tp')
- conv_query_grad: float32 [3, 768], replicated
- conv_key_grad: float32 [3, 768], replicated
- conv_value_grad: float32 [3, 768], replicated
- w_out_grad: float32 [768, 768], P('tp', 'fsdp')
- ln2_gain_grad: float32 [768], replicated
- ln2_bias_grad: float32 [768], replicated
- w_up_grad: float32 [768, 3072], P('fsdp', 'tp')
- up_bias_grad: float32 [3072], replicated
- w_down_grad: float32 [3072, 768], P('tp', 'fsdp')
- down_bias_grad: float32 [768], replicated
All inputs are finite; a program needn't handle non-finite values.
Results may differ from a plain program's by a relative error of at most 0.02.
Values may be sent and summed in bfloat16 or wider, within the bound.
A program may use at most 192 MiB of HBM per device.

v0:
```python
import jax
import jax.numpy as jnp
from jax import lax
from jax.sharding import PartitionSpec as P

HEAD_DIM = 64
D = 768
FF = 3072
KBLOCK = 256
QBLOCK = 512
EPS = 1e-05
MASKED = -1e30


def normalize(values, gain, shift):
    center = values - jnp.mean(values, axis=-1, keepdims=True)
    inverse = lax.rsqrt(jnp.mean(center * center, axis=-1, keepdims=True) + EPS)
    unit = center * inverse
    return (unit, inverse, unit * gain + shift)


def normalize_back(grad_rows, unit, inverse, gain):
    scaled = grad_rows * gain
    return inverse * (
        scaled
        - jnp.mean(scaled, axis=-1, keepdims=True)
        - unit * jnp.mean(scaled * unit, axis=-1, keepdims=True)
    )


def shifted(values, steps):
    return jnp.concatenate(
        [jnp.zeros((steps, values.shape[1]), values.dtype), values[:-steps]], axis=0
    )


def advanced(values, steps):
    return jnp.concatenate(
        [values[steps:], jnp.zeros((steps, values.shape[1]), values.dtype)], axis=0
    )


def conv_apply(values, kernel):
    return kernel[0] * values + kernel[1] * shifted(values, 1) + kernel[2] * shifted(values, 2)


def conv_back(grad_mix, values, kernel):
    grad_values = (
        kernel[0] * grad_mix + kernel[1] * advanced(grad_mix, 1) + kernel[2] * advanced(grad_mix, 2)
    )
    kernel_grad = jnp.stack(
        [
            jnp.sum(grad_mix * values, axis=0),
            jnp.sum(grad_mix * shifted(values, 1), axis=0),
            jnp.sum(grad_mix * shifted(values, 2), axis=0),
        ]
    )
    return (grad_values, kernel_grad)


def block_scores(query_part, key_part, first):
    rows = query_part.shape[0]
    keys = key_part.shape[0]
    row_block = (first + jnp.arange(rows, dtype=jnp.int32)) // KBLOCK
    key_block = jnp.arange(keys, dtype=jnp.int32) // KBLOCK
    allowed = key_block[None, :] <= row_block[:, None]
    raw = jnp.einsum(
        "qhd,khd->hqk", query_part, key_part, preferred_element_type=jnp.float32
    ) * HEAD_DIM ** (-0.5)
    return jnp.where(allowed[None], raw, MASKED)


def attend(query_mix, key_mix, value_mix):
    length = query_mix.shape[0]
    outputs = []
    totals = []
    for first in range(0, length, QBLOCK):
        final = first + QBLOCK
        scores = block_scores(query_mix[first:final], key_mix[:final], first)
        top_score = jnp.max(scores, axis=-1, keepdims=True)
        log_total = top_score + jnp.log(
            jnp.sum(jnp.exp(scores - top_score), axis=-1, keepdims=True)
        )
        weights = jnp.exp(scores - log_total).astype(jnp.bfloat16)
        outputs.append(
            jnp.einsum(
                "hqk,khd->qhd", weights, value_mix[:final], preferred_element_type=jnp.float32
            )
        )
        totals.append(log_total)
    return (jnp.concatenate(outputs, axis=0), totals)


def attend_back(query_mix, key_mix, value_mix, grad_mixed, totals):
    length = query_mix.shape[0]
    grad_query = []
    grad_key = jnp.zeros(key_mix.shape, jnp.float32)
    grad_value = jnp.zeros(value_mix.shape, jnp.float32)
    for number, first in enumerate(range(0, length, QBLOCK)):
        final = first + QBLOCK
        scores = block_scores(query_mix[first:final], key_mix[:final], first)
        exact = jnp.exp(scores - totals[number])
        rounded = exact.astype(jnp.bfloat16)
        grad_weights = jnp.einsum(
            "qhd,khd->hqk",
            grad_mixed[first:final],
            value_mix[:final],
            preferred_element_type=jnp.float32,
        )
        inner = jnp.sum(exact * grad_weights, axis=-1, keepdims=True)
        grad_scores = (exact * (grad_weights - inner)).astype(jnp.bfloat16)
        grad_query.append(
            jnp.einsum(
                "hqk,khd->qhd", grad_scores, key_mix[:final], preferred_element_type=jnp.float32
            )
            * HEAD_DIM ** (-0.5)
        )
        grad_key = grad_key.at[:final].add(
            jnp.einsum(
                "hqk,qhd->khd",
                grad_scores,
                query_mix[first:final],
                preferred_element_type=jnp.float32,
            )
            * HEAD_DIM ** (-0.5)
        )
        grad_value = grad_value.at[:final].add(
            jnp.einsum(
                "hqk,qhd->khd", rounded, grad_mixed[first:final], preferred_element_type=jnp.float32
            )
        )
    return (jnp.concatenate(grad_query, axis=0), grad_key, grad_value)


def fetch(shards):
    return (
        lax.all_gather(shards[0], "fsdp", axis=0, tiled=True),
        lax.all_gather(shards[1], "fsdp", axis=0, tiled=True),
        lax.all_gather(shards[2], "fsdp", axis=0, tiled=True),
        lax.all_gather(shards[3], "fsdp", axis=1, tiled=True),
        lax.all_gather(shards[4], "fsdp", axis=0, tiled=True),
        lax.all_gather(shards[5], "fsdp", axis=1, tiled=True),
    )


def settle(grads):
    return (
        lax.psum_scatter(grads[0], "fsdp", scatter_dimension=0, tiled=True),
        lax.psum_scatter(grads[1], "fsdp", scatter_dimension=0, tiled=True),
        lax.psum_scatter(grads[2], "fsdp", scatter_dimension=0, tiled=True),
        lax.psum_scatter(grads[3], "fsdp", scatter_dimension=1, tiled=True),
        lax.psum_scatter(grads[4], "fsdp", scatter_dimension=0, tiled=True),
        lax.psum_scatter(grads[5], "fsdp", scatter_dimension=1, tiled=True),
    )


def rows_in(piece):
    return lax.all_gather(piece, "tp", axis=0, tiled=True)


def rows_out(term, rows):
    return lax.psum_scatter(
        term(jnp.int32(0), lax.axis_size("tp") * rows).astype(jnp.bfloat16),
        "tp",
        scatter_dimension=0,
        tiled=True,
    ).astype(jnp.float32)


def local(
    layer_input,
    out_grad,
    ln1_gain,
    ln1_bias,
    w_query,
    w_key,
    w_value,
    conv_query,
    conv_key,
    conv_value,
    w_out,
    ln2_gain,
    ln2_bias,
    w_up,
    up_bias,
    w_down,
    down_bias,
):
    rank = lax.axis_index("tp")
    width = w_query.shape[1]
    units = w_up.shape[1]
    heads = width // HEAD_DIM
    kern_query = lax.dynamic_slice_in_dim(conv_query, rank * width, width, 1)
    kern_key = lax.dynamic_slice_in_dim(conv_key, rank * width, width, 1)
    kern_value = lax.dynamic_slice_in_dim(conv_value, rank * width, width, 1)
    bias_up = lax.dynamic_slice_in_dim(up_bias, rank * units, units, 0)
    shards = (w_query, w_key, w_value, w_out, w_up, w_down)
    owned_grads = tuple((jnp.zeros(item.shape, jnp.float32) for item in shards))
    vector_zero = jnp.zeros((D,), jnp.float32)
    gain_one, shift_one, gain_two, shift_two, bias_down_grad = (
        vector_zero,
        vector_zero,
        vector_zero,
        vector_zero,
        vector_zero,
    )
    kernel_zero = jnp.zeros((3, width), jnp.float32)
    query_kernel_grad, key_kernel_grad, value_kernel_grad = (kernel_zero, kernel_zero, kernel_zero)
    bias_up_grad = jnp.zeros((units,), jnp.float32)
    results = []
    input_grads = []
    for micro_step in range(layer_input.shape[0]):
        gathered = fetch(shards)
        full_query, full_key, full_value, full_out, full_up, full_down = gathered
        piece = layer_input[micro_step].astype(jnp.float32)
        rows = piece.shape[0]
        unit_one, inverse_one, normed_one = normalize(piece, ln1_gain, ln1_bias)
        hidden_one = rows_in(normed_one.astype(jnp.bfloat16))
        proj_query = jnp.dot(hidden_one, full_query, preferred_element_type=jnp.float32)
        proj_key = jnp.dot(hidden_one, full_key, preferred_element_type=jnp.float32)
        proj_value = jnp.dot(hidden_one, full_value, preferred_element_type=jnp.float32)
        query_mix = (
            conv_apply(proj_query, kern_query).astype(jnp.bfloat16).reshape(-1, heads, HEAD_DIM)
        )
        key_mix = conv_apply(proj_key, kern_key).astype(jnp.bfloat16).reshape(-1, heads, HEAD_DIM)
        value_mix = (
            conv_apply(proj_value, kern_value).astype(jnp.bfloat16).reshape(-1, heads, HEAD_DIM)
        )
        mixed, totals = attend(query_mix, key_mix, value_mix)
        attn_rows = mixed.reshape(-1, width).astype(jnp.bfloat16)

        def attn_term(start, count):
            return jnp.dot(attn_rows, full_out, preferred_element_type=jnp.float32)

        resid = piece + rows_out(attn_term, rows)
        unit_two, inverse_two, normed_two = normalize(resid, ln2_gain, ln2_bias)
        hidden_two = rows_in(normed_two.astype(jnp.bfloat16))
        pre_act = jnp.dot(hidden_two, full_up, preferred_element_type=jnp.float32) + bias_up
        relu_part = jnp.maximum(pre_act, 0.0)
        activ = (relu_part * relu_part).astype(jnp.bfloat16)

        def ffn_term(start, count):
            return jnp.dot(activ, full_down, preferred_element_type=jnp.float32)

        results.append((resid + rows_out(ffn_term, rows) + down_bias).astype(jnp.bfloat16))
        gathered = fetch(shards)
        full_query, full_key, full_value, full_out, full_up, full_down = gathered
        grad_top = out_grad[micro_step].astype(jnp.float32)
        bias_down_grad = bias_down_grad + jnp.sum(grad_top, axis=0)
        grad_ffn = rows_in(out_grad[micro_step])
        down_local = jnp.einsum("tu,td->ud", activ, grad_ffn, preferred_element_type=jnp.float32)
        grad_act = jnp.einsum("td,ud->tu", grad_ffn, full_down, preferred_element_type=jnp.float32)
        grad_pre = (grad_act * 2.0 * relu_part).astype(jnp.bfloat16)
        bias_up_grad = bias_up_grad + jnp.sum(grad_pre.astype(jnp.float32), axis=0)
        up_local = jnp.einsum("td,tu->du", hidden_two, grad_pre, preferred_element_type=jnp.float32)

        def up_term(start, count):
            return jnp.einsum("tu,du->td", grad_pre, full_up, preferred_element_type=jnp.float32)

        grad_normed_two = rows_out(up_term, rows)
        gain_two = gain_two + jnp.sum(grad_normed_two * unit_two, axis=0)
        shift_two = shift_two + jnp.sum(grad_normed_two, axis=0)
        grad_resid = grad_top + normalize_back(grad_normed_two, unit_two, inverse_two, ln2_gain)
        grad_attn = rows_in(grad_resid.astype(jnp.bfloat16))
        out_local = jnp.einsum(
            "tc,td->cd", attn_rows, grad_attn, preferred_element_type=jnp.float32
        )
        grad_mixed = (
            jnp.einsum("td,cd->tc", grad_attn, full_out, preferred_element_type=jnp.float32)
            .astype(jnp.bfloat16)
            .reshape(-1, heads, HEAD_DIM)
        )
        grad_qmix, grad_kmix, grad_vmix = attend_back(
            query_mix, key_mix, value_mix, grad_mixed, totals
        )
        grad_query, query_tap = conv_back(grad_qmix.reshape(-1, width), proj_query, kern_query)
        grad_key, key_tap = conv_back(grad_kmix.reshape(-1, width), proj_key, kern_key)
        grad_value, value_tap = conv_back(grad_vmix.reshape(-1, width), proj_value, kern_value)
        query_kernel_grad = query_kernel_grad + query_tap
        key_kernel_grad = key_kernel_grad + key_tap
        value_kernel_grad = value_kernel_grad + value_tap
        grad_query = grad_query.astype(jnp.bfloat16)
        grad_key = grad_key.astype(jnp.bfloat16)
        grad_value = grad_value.astype(jnp.bfloat16)
        query_local = jnp.einsum(
            "td,tc->dc", hidden_one, grad_query, preferred_element_type=jnp.float32
        )
        key_local = jnp.einsum(
            "td,tc->dc", hidden_one, grad_key, preferred_element_type=jnp.float32
        )
        value_local = jnp.einsum(
            "td,tc->dc", hidden_one, grad_value, preferred_element_type=jnp.float32
        )

        def input_term(start, count):
            total = jnp.einsum(
                "tc,dc->td", grad_query, full_query, preferred_element_type=jnp.float32
            )
            total = total + jnp.einsum(
                "tc,dc->td", grad_key, full_key, preferred_element_type=jnp.float32
            )
            return total + jnp.einsum(
                "tc,dc->td", grad_value, full_value, preferred_element_type=jnp.float32
            )

        grad_normed_one = rows_out(input_term, rows)
        gain_one = gain_one + jnp.sum(grad_normed_one * unit_one, axis=0)
        shift_one = shift_one + jnp.sum(grad_normed_one, axis=0)
        input_grads.append(
            (grad_resid + normalize_back(grad_normed_one, unit_one, inverse_one, ln1_gain)).astype(
                jnp.bfloat16
            )
        )
        step_grads = (query_local, key_local, value_local, out_local, up_local, down_local)
        owned_grads = jax.tree.map(jnp.add, owned_grads, settle(step_grads))
    kernel_full = jnp.zeros((3, D), jnp.float32)
    query_kernel_full = lax.dynamic_update_slice_in_dim(
        kernel_full, query_kernel_grad, rank * width, 1
    )
    key_kernel_full = lax.dynamic_update_slice_in_dim(kernel_full, key_kernel_grad, rank * width, 1)
    value_kernel_full = lax.dynamic_update_slice_in_dim(
        kernel_full, value_kernel_grad, rank * width, 1
    )
    bias_up_full = lax.dynamic_update_slice_in_dim(
        jnp.zeros((FF,), jnp.float32), bias_up_grad, rank * units, 0
    )
    summed = lax.psum(
        (
            gain_one,
            shift_one,
            query_kernel_full,
            key_kernel_full,
            value_kernel_full,
            gain_two,
            shift_two,
            bias_up_full,
            bias_down_grad,
        ),
        ("fsdp", "tp"),
    )
    return (
        jnp.stack(results),
        jnp.stack(input_grads),
        summed[0],
        summed[1],
        owned_grads[0],
        owned_grads[1],
        owned_grads[2],
        summed[2],
        summed[3],
        summed[4],
        owned_grads[3],
        summed[5],
        summed[6],
        owned_grads[4],
        summed[7],
        owned_grads[5],
        summed[8],
    )


def solution(mesh):
    return jax.shard_map(
        local,
        mesh=mesh,
        in_specs=(
            P(None, ("fsdp", "tp"), None),
            P(None, ("fsdp", "tp"), None),
            P(),
            P(),
            P("fsdp", "tp"),
            P("fsdp", "tp"),
            P("fsdp", "tp"),
            P(),
            P(),
            P(),
            P("tp", "fsdp"),
            P(),
            P(),
            P("fsdp", "tp"),
            P(),
            P("tp", "fsdp"),
            P(),
        ),
        out_specs=(
            P(None, ("fsdp", "tp"), None),
            P(None, ("fsdp", "tp"), None),
            P(),
            P(),
            P("fsdp", "tp"),
            P("fsdp", "tp"),
            P("fsdp", "tp"),
            P(),
            P(),
            P(),
            P("tp", "fsdp"),
            P(),
            P(),
            P("fsdp", "tp"),
            P(),
            P("tp", "fsdp"),
            P(),
        ),
        check_vma=False,
    )
```

profile of v0, /device:TPU:0, one launch (start us, length us, event | category | flops | bytes accessed | tf_op | source)
XLA Modules:
  0.0 1096.2 jit_solution(10316709794128129012)
XLA Ops:
  15.6 35.0 %all_gather.64 = bf16[192,768]{0,1:T(8,128)(2,1)} all-gather(bf16[192,96]{0,1:T(8,128)(2,1)S(1)} %copy.43), channel_id=1, replica_groups=mesh['fsdp'=8,'tp'=4] {'fsdp'}, dimensions={1}, use_global_device_ids=true | all-gather | bytes 331776 | tf_op jit(solution)/shard_map/all_gather | solution.py:140
  50.6 33.2 %all_gather.30 = bf16[768,192]{1,0:T(8,128)(2,1)} all-gather(bf16[96,192]{1,0:T(8,128)(2,1)} %param.45), channel_id=1, replica_groups=mesh['fsdp'=8,'tp'=4] {'fsdp'}, dimensions={0}, use_global_device_ids=true | all-gather | bytes 331776 | tf_op jit(solution)/shard_map/all_gather | solution.py:137
  83.8 31.0 %all_gather.31 = bf16[768,192]{1,0:T(8,128)(2,1)S(1)} all-gather(bf16[96,192]{1,0:T(8,128)(2,1)S(1)} %copy-done.120), channel_id=1, replica_groups=mesh['fsdp'=8,'tp'=4] {'fsdp'}, dimensions={0}, use_global_device_ids=true | all-gather | bytes 331776 | tf_op jit(solution)/shard_map/all_gather | solution.py:138
  114.8 33.2 %all_gather.29 = bf16[768,192]{1,0:T(8,128)(2,1)} all-gather(bf16[96,192]{1,0:T(8,128)(2,1)S(1)} %copy-done.121), channel_id=1, replica_groups=mesh['fsdp'=8,'tp'=4] {'fsdp'}, dimensions={0}, use_global_device_ids=true | all-gather | bytes 331776 | tf_op jit(solution)/shard_map/all_gather | solution.py:139
  165.9 29.3 %reduce-scatter.17.cloned.1.call-done = bf16[256,768]{1,0:T(8,128)(2,1)} async-done(((bf16[1024,768]{1,0:T(8,128)(2,1)}), bf16[256,768]{1,0:T(8,128)(2,1)}) %reduce-scatter.17.cloned.1.call-update) | async-done | bytes 393232 | tf_op jit(solution)/shard_map/reduce_scatter | solution.py:162
  198.2 19.7 %all-gather.21.cloned.1.call-done = bf16[1024,768]{1,0:T(8,128)(2,1)} async-done(((bf16[256,768]{1,0:T(8,128)(2,1)}), bf16[1024,768]{1,0:T(8,128)(2,1)}) %all-gather.21.cloned.1.call-update) | async-done | bytes 1572880 | tf_op jit(solution)/shard_map/all_gather | solution.py:158
  237.3 26.3 %reduce-scatter.21.cloned.1.call-done = bf16[256,768]{1,0:T(8,128)(2,1)} async-done(((bf16[1024,768]{1,0:T(8,128)(2,1)}), bf16[256,768]{1,0:T(8,128)(2,1)}) %reduce-scatter.21.cloned.1.call-update) | async-done | bytes 393232 | tf_op jit(solution)/shard_map/reduce_scatter | solution.py:162
  279.4 19.3 %all-gather.23.cloned.1.call-done = bf16[1024,768]{1,0:T(8,128)(2,1)} async-done(((bf16[256,768]{1,0:T(8,128)(2,1)}), bf16[1024,768]{1,0:T(8,128)(2,1)}) %all-gather.23.cloned.1.call-update) | async-done | bytes 1572880 | tf_op jit(solution)/shard_map/all_gather | solution.py:158
  303.5 38.7 %all-gather.19.cloned.1.call-done = bf16[768,768]{0,1:T(8,128)(2,1)} async-done(((bf16[768,96]{0,1:T(8,128)(2,1)}), bf16[768,768]{0,1:T(8,128)(2,1)}) %all-gather.19.cloned.1.call-update) | async-done | bytes 1179664 | tf_op jit(solution)/shard_map/all_gather | solution.py:142
  342.2 19.5 %all-gather.31.cloned.1.call-done = bf16[1,1024,768]{2,1,0:T(8,128)(2,1)} async-done(((bf16[1,256,768]{2,1,0:T(8,128)(2,1)}), bf16[1,1024,768]{2,1,0:T(8,128)(2,1)}) %all-gather.31.cloned.1.call-update) | async-done | bytes 1572880 | tf_op jit(solution)/shard_map/all_gather | solution.py:158
  370.4 13.0 %all-gather.15.cloned.1.call-done = bf16[1024,768]{1,0:T(8,128)(2,1)} async-done(((bf16[256,768]{1,0:T(8,128)(2,1)}), bf16[1024,768]{1,0:T(8,128)(2,1)}) %all-gather.15.cloned.1.call-update) | async-done | bytes 1572880 | tf_op jit(solution)/shard_map/all_gather | solution.py:158
  388.2 19.1 %all-gather.29.cloned.1.call-done = bf16[1,1024,768]{2,1,0:T(8,128)(2,1)} async-done(((bf16[1,256,768]{2,1,0:T(8,128)(2,1)}), bf16[1,1024,768]{2,1,0:T(8,128)(2,1)}) %all-gather.29.cloned.1.call-update) | async-done | bytes 1572880 | tf_op jit(solution)/shard_map/all_gather | solution.py:158
  415.9 28.1 %reduce-scatter.25.cloned.1.call-done = bf16[256,768]{1,0:T(8,128)(2,1)} async-done(((bf16[1024,768]{1,0:T(8,128)(2,1)}), bf16[256,768]{1,0:T(8,128)(2,1)}) %reduce-scatter.25.cloned.1.call-update) | async-done | bytes 393232 | tf_op jit(solution)/shard_map/reduce_scatter | solution.py:162
  451.5 18.6 %all-gather.27.cloned.1.call-done = bf16[1024,768]{1,0:T(8,128)(2,1)} async-done(((bf16[256,768]{1,0:T(8,128)(2,1)}), bf16[1024,768]{1,0:T(8,128)(2,1)}) %all-gather.27.cloned.1.call-update) | async-done | bytes 1572880 | tf_op jit(solution)/shard_map/all_gather | solution.py:158
  481.6 9.9 all-gather.25.cloned.1.call-done
  634.7 16.1 %reduce-scatter.31.cloned.1.call-done = bf16[256,768]{1,0:T(8,128)(2,1)} async-done(((bf16[1024,768]{1,0:T(8,128)(2,1)}), bf16[256,768]{1,0:T(8,128)(2,1)}) %reduce-scatter.31.cloned.1.call-update) | async-done | bytes 393232 | tf_op jit(solution)/shard_map/reduce_scatter | solution.py:162
  650.8 30.4 %reduce-scatter.27.cloned.1.call-done = bf16[256,768]{1,0:T(8,128)(2,1)} async-done(((bf16[1024,768]{1,0:T(8,128)(2,1)}), bf16[256,768]{1,0:T(8,128)(2,1)}) %reduce-scatter.27.cloned.1.call-update) | async-done | bytes 393232 | tf_op jit(solution)/shard_map/reduce_scatter | solution.py:162
  686.7 41.9 %all-reduce.28 = (f32[768]{0:T(1024)}, f32[768]{0:T(1024)}, f32[3,768]{1,0:T(4,128)}, f32[3,768]{1,0:T(4,128)}, f32[3,768]{1,0:T(4,128)}, /*index=5*/f32[768]{0:...) all-reduce(f32[768]{0:T(1024)} %add.555, ...), channel_id=1, replica_groups=mesh['fsdp'=8,'tp'=4] {'fsdp','tp'}, use_global_device_ids=true, to_apply=%region_38.39 | all-reduce | flops 13824 | bytes 110592 | tf_op jit(solution)/shard_map/psum | solution.py:327
  732.9 9.2 reduce-scatter.19.cloned.1.call-done
  745.9 70.2 %reduce-scatter.41.cloned.1.call-done = f32[768,96]{0,1:T(8,128)} async-done(((f32[768,768]{0,1:T(8,128)}), f32[768,96]{0,1:T(8,128)}) %reduce-scatter.41.cloned.1.call-update) | async-done | bytes 294928 | tf_op jit(solution)/shard_map/reduce_scatter | solution.py:153
  816.0 73.3 %reduce-scatter.39.cloned.1.call-done = f32[96,768]{1,0:T(8,128)} async-done(((f32[768,768]{1,0:T(8,128)}), f32[96,768]{1,0:T(8,128)}) %reduce-scatter.39.cloned.1.call-update) | async-done | bytes 294928 | tf_op jit(solution)/shard_map/reduce_scatter | solution.py:152
  889.3 66.4 %reduce-scatter.37.cloned.1.call-done = f32[96,192]{1,0:T(8,128)} async-done(((f32[768,192]{1,0:T(8,128)}), f32[96,192]{1,0:T(8,128)}) %reduce-scatter.37.cloned.1.call-update) | async-done | bytes 73744 | tf_op jit(solution)/shard_map/reduce_scatter | solution.py:150
  955.7 66.3 %reduce-scatter.35.cloned.1.call-done = f32[96,192]{1,0:T(8,128)} async-done(((f32[768,192]{1,0:T(8,128)}), f32[96,192]{1,0:T(8,128)}) %reduce-scatter.35.cloned.1.call-update) | async-done | bytes 73744 | tf_op jit(solution)/shard_map/reduce_scatter | solution.py:149
  1022.0 66.2 %reduce-scatter.33.cloned.1.call-done = f32[96,192]{1,0:T(8,128)} async-done(((f32[768,192]{1,0:T(8,128)}), f32[96,192]{1,0:T(8,128)}) %reduce-scatter.33.cloned.1.call-update) | async-done | bytes 73744 | tf_op jit(solution)/shard_map/reduce_scatter | solution.py:148
  (556 shorter events, 263.9 us)
Async XLA Ops:
  8.0 141.3 %all-gather.13.cloned.1.call-start = ((), (), s32[]{:S(2)}) async-start(), calls=%async_computation.14 | async-start | bytes 1966080 | tf_op jit(solution)/shard_map/all_gather | solution.py:158
  12.7 182.5 %reduce-scatter.17.cloned.1.call-start = ((), (), s32[]{:S(2)}) async-start(), calls=%async_computation.15 | async-start | bytes 1966080 | tf_op jit(solution)/shard_map/reduce_scatter | solution.py:162
  165.7 52.2 %all-gather.21.cloned.1.call-start = ((), (), s32[]{:S(2)}) async-start(), calls=%async_computation.20 | async-start | bytes 1966080 | tf_op jit(solution)/shard_map/all_gather | solution.py:158
  198.1 65.5 %reduce-scatter.21.cloned.1.call-start = ((), (), s32[]{:S(2)}) async-start(), calls=%async_computation.21 | async-start | bytes 1966080 | tf_op jit(solution)/shard_map/reduce_scatter | solution.py:162
  235.4 44.0 %all-gather.17.cloned.1.call-start = ((), (), s32[]{:S(2)}) async-start(), calls=%async_computation.17 | async-start | bytes 1327104 | tf_op jit(solution)/shard_map/all_gather | solution.py:141
  236.0 62.7 %all-gather.23.cloned.1.call-start = ((), (), s32[]{:S(2)}) async-start(), calls=%async_computation.22 | async-start | bytes 1966080 | tf_op jit(solution)/shard_map/all_gather | solution.py:158
  268.6 73.6 %all-gather.19.cloned.1.call-start = ((), (), s32[]{:S(2)}) async-start(), calls=%async_computation.18 | async-start | bytes 1327104 | tf_op jit(solution)/shard_map/all_gather | solution.py:142
  269.2 92.5 %all-gather.31.cloned.1.call-start = ((), (), s32[]{:S(2)}) async-start(), calls=%async_computation.31 | async-start | bytes 1966080 | tf_op jit(solution)/shard_map/all_gather | solution.py:158
  271.4 112.0 %all-gather.15.cloned.1.call-start = ((), (), s32[]{:S(2)}) async-start(), calls=%async_computation.16 | async-start | bytes 1966080 | tf_op jit(solution)/shard_map/all_gather | solution.py:158
  272.1 135.1 %all-gather.29.cloned.1.call-start = ((), (), s32[]{:S(2)}) async-start(), calls=%async_computation.30 | async-start | bytes 1966080 | tf_op jit(solution)/shard_map/all_gather | solution.py:158
  272.9 143.1 %reduce-scatter.29.cloned.1.call-start = ((), (), s32[]{:S(2)}) async-start(), calls=%async_computation.27 | async-start | bytes 1966080 | tf_op jit(solution)/shard_map/reduce_scatter | solution.py:162
  370.4 73.7 %reduce-scatter.25.cloned.1.call-start = ((), (), s32[]{:S(2)}) async-start(), calls=%async_computation.24 | async-start | bytes 1966080 | tf_op jit(solution)/shard_map/reduce_scatter | solution.py:162
  415.9 54.2 %all-gather.27.cloned.1.call-start = ((), (), s32[]{:S(2)}) async-start(), calls=%async_computation.28 | async-start | bytes 1966080 | tf_op jit(solution)/shard_map/all_gather | solution.py:158
  450.4 41.1 %all-gather.25.cloned.1.call-start = ((), (), s32[]{:S(2)}) async-start(), calls=%async_computation.25 | async-start | bytes 1966080 | tf_op jit(solution)/shard_map/all_gather | solution.py:158
  451.0 182.0 %reduce-scatter.43.cloned.1.call-start = ((), (), s32[]{:S(2)}) async-start(), calls=%async_computation.37 | async-start | bytes 884736
  557.7 93.1 %reduce-scatter.31.cloned.1.call-start = ((), (), s32[]{:S(2)}) async-start(), calls=%async_computation.29 | async-start | bytes 1966080 | tf_op jit(solution)/shard_map/reduce_scatter | solution.py:162
  569.0 112.2 %reduce-scatter.27.cloned.1.call-start = ((), (), s32[]{:S(2)}) async-start(), calls=%async_computation.26 | async-start | bytes 1966080 | tf_op jit(solution)/shard_map/reduce_scatter | solution.py:162
  573.6 156.4 %reduce-scatter.23.cloned.1.call-start = ((), (), s32[]{:S(2)}) async-start(), calls=%async_computation.23 | async-start | bytes 1966080 | tf_op jit(solution)/shard_map/reduce_scatter | solution.py:162
  578.5 163.7 %reduce-scatter.19.cloned.1.call-start = ((), (), s32[]{:S(2)}) async-start(), calls=%async_computation.19 | async-start | bytes 1966080 | tf_op jit(solution)/shard_map/reduce_scatter | solution.py:162
  583.4 232.7 %reduce-scatter.41.cloned.1.call-start = ((), (), s32[]{:S(2)}) async-start(), calls=%async_computation.36 | async-start | bytes 2654208 | tf_op jit(solution)/shard_map/reduce_scatter | solution.py:153
  590.6 298.7 %reduce-scatter.39.cloned.1.call-start = ((), (), s32[]{:S(2)}) async-start(), calls=%async_computation.35 | async-start | bytes 2654208 | tf_op jit(solution)/shard_map/reduce_scatter | solution.py:152
  597.4 358.3 %reduce-scatter.37.cloned.1.call-start = ((), (), s32[]{:S(2)}) async-start(), calls=%async_computation.34 | async-start | bytes 884736 | tf_op jit(solution)/shard_map/reduce_scatter | solution.py:150
  608.7 413.3 %reduce-scatter.35.cloned.1.call-start = ((), (), s32[]{:S(2)}) async-start(), calls=%async_computation.33 | async-start | bytes 884736 | tf_op jit(solution)/shard_map/reduce_scatter | solution.py:149
  620.9 467.3 %reduce-scatter.33.cloned.1.call-start = ((), (), s32[]{:S(2)}) async-start(), calls=%async_computation.32 | async-start | bytes 884736 | tf_op jit(solution)/shard_map/reduce_scatter | solution.py:148
  (166 other events, 3785.8 us)
Sparse Core Ops, SparseCore 0:
  12.8 22.3 all-gather.12
  165.8 29.3 reduce-scatter.16
  198.2 19.6 all-gather.20
  235.5 28.0 reduce-scatter.20
  370.5 28.3 reduce-scatter.28
  416.0 27.9 reduce-scatter.24
Sparse Core Ops, SparseCore 1:
  238.1 41.3 all-gather.16
  280.9 17.8 all-gather.22
  300.8 41.4 all-gather.18
  343.8 17.8 all-gather.30
  363.9 19.5 all-gather.14
  385.0 22.2 all-gather.28
  450.5 19.5 all-gather.26
  472.0 19.5 all-gather.24
  557.8 63.4 reduce-scatter.42
  623.8 26.9 reduce-scatter.30
  653.3 27.9 reduce-scatter.26
  683.8 28.0 reduce-scatter.22
  714.3 27.8 reduce-scatter.18
  746.3 69.7 reduce-scatter.40
  820.1 69.1 reduce-scatter.38
  893.2 62.4 reduce-scatter.36
  959.6 62.3 reduce-scatter.34
  1025.9 62.3 reduce-scatter.32
where the time goes:
time: 1110 us; the launch traced here: 1100 us
  waiting for transfers between devices  648 us (58%)
  blocking collectives  174 us (16%)
  matrix products  132 us (12%)
  other arithmetic  90.4 us (8%)
  local copies, waits for them, and re-layouts  30.4 us (3%)
  between operations  18.5 us (2%)
    reduce_scatter x8, waiting for transfers between devices, rows_out(): lax.psum_scatter(term(jnp.int32(0), lax.axis_size('tp') * rows).astype(jn...  139 us
    all_gather x8, waiting for transfers between devices, rows_in(): return lax.all_gather(piece, 'tp', axis=0, tiled=True)  119 us
    reduce_scatter x1, waiting for transfers between devices, settle(): lax.psum_scatter(grads[4], 'fsdp', scatter_dimension=0, tiled=True)  73.3 us
    reduce_scatter x1, waiting for transfers between devices, settle(): lax.psum_scatter(grads[5], 'fsdp', scatter_dimension=1, tiled=True)  70.2 us
    reduce_scatter x1, waiting for transfers between devices, settle(): lax.psum_scatter(grads[2], 'fsdp', scatter_dimension=0, tiled=True)  66.4 us
    reduce_scatter x1, waiting for transfers between devices, settle(): lax.psum_scatter(grads[1], 'fsdp', scatter_dimension=0, tiled=True)  66.3 us
    reduce_scatter x1, waiting for transfers between devices, settle(): lax.psum_scatter(grads[0], 'fsdp', scatter_dimension=0, tiled=True)  66.2 us
    psum x1, blocking collectives, local(): lax.psum((gain_one, shift_one, query_kernel_full, key_kernel_full, value_...  41.9 us
  transfers between devices with their start and end apart: 24, of which 20 were waited for; matrix products, arithmetic and copies ran while one was open for 12% of the time, Pallas kernels for 0%

commit v1 on v0

--- a/solution.py
+++ b/solution.py
@@ -10,6 +10,44 @@
 QBLOCK = 512
 EPS = 1e-05
 MASKED = -1e30
+
+
+def name_the_roads(field, chip_axis, on_dim):
+    step_out, x_now, r_now = (
+        jax.lax.axis_size(chip_axis),
+        jax.lax.axis_index(chip_axis),
+        field.shape[on_dim],
+    )
+    runs = []
+    for b, ii in enumerate(field.shape):
+        runs.append(ii * step_out if b == on_dim else ii)
+    back = lax.dynamic_update_slice_in_dim(
+        jnp.zeros(runs, field.dtype), field, x_now * r_now, axis=on_dim
+    )
+    item_now = local_part = field
+    nth = 1
+    while nth < step_out // 2 + 1:
+        items = []
+        b = 0
+        while b < step_out:
+            items.append((b, (b + 1) % step_out))
+            b = b + 1
+        item_now = jax.lax.ppermute(item_now, axis_name=chip_axis, perm=items)
+        back = lax.dynamic_update_slice_in_dim(
+            back, item_now, (x_now - nth) % step_out * r_now, axis=on_dim
+        )
+        if 2 * nth < step_out:
+            grid = []
+            b = 0
+            while b < step_out:
+                grid.append((b, (b - 1) % step_out))
+                b += 1
+            local_part = jax.lax.ppermute(local_part, axis_name=chip_axis, perm=grid)
+            back = lax.dynamic_update_slice_in_dim(
+                back, local_part, (x_now + nth) % step_out * r_now, axis=on_dim
+            )
+        nth += 1
+    return back
 
 
 def normalize(values, gain, shift):
@@ -155,7 +193,7 @@
 
 
 def rows_in(piece):
-    return lax.all_gather(piece, "tp", axis=0, tiled=True)
+    return name_the_roads(piece, "tp", 0)
 
 
 def rows_out(term, rows):

time: 1110 us -> 1040 us (0.937)
  waiting for transfers between devices: 648 us -> 583 us
  matrix products: 132 us -> 113 us
  local copies, waits for them, and re-layouts: 30.4 us -> 46.1 us
  starting transfers between devices: 2.57 us -> 17.3 us
    all_gather x8 -> x0, waiting for transfers between devices: 119 us -> none  [rows_in(): return lax.all_gather(piece, 'tp', axis=0, tiled=True)]
    ppermute x0 -> x24, waiting for transfers between devices: none -> 78.4 us  [the longest x16 76.3 us: name_the_roads(): item_now = jax.lax.ppermute(item_now, axis_name=chip_axis, perm=items)]
    all_gather x1, waiting for transfers between devices: 38.7 us -> 21.5 us  [fetch(): lax.all_gather(shards[5], 'fsdp', axis=1, tiled=True)]
    ppermute x0 -> x24, starting transfers between devices: none -> 15.8 us  [the longest x8 10.9 us: name_the_roads(): local_part = jax.lax.ppermute(local_part, axis_name=chip_axis, perm=grid)]
    dynamic_update_slice x0 -> x26, local copies, waits for them, and re-layouts: none -> 12.2 us  [the longest x16 7.64 us: name_the_roads(): lax.dynamic_update_slice_in_dim(back, item_now, (x_now - nth) % step_out...]
  transfers between devices with their start and end apart: 24 -> 40, of which waited for: 20 -> 27; matrix products, arithmetic and copies ran while one was open for 12% -> 12% of each run, Pallas kernels for 0% -> 0%
where the time goes in v1:
time: 1040 us; the launch traced here: 1030 us
  waiting for transfers between devices  583 us (56%)
  blocking collectives  170 us (16%)
  matrix products  113 us (11%)
  other arithmetic  85.8 us (8%)
  local copies, waits for them, and re-layouts  46.1 us (4%)
  between operations  18.5 us (2%)
  starting transfers between devices  17.3 us (2%)
    reduce_scatter x8, waiting for transfers between devices, rows_out(): lax.psum_scatter(term(jnp.int32(0), lax.axis_size('tp') * rows).astype(jn...  140 us
    ppermute x16, waiting for transfers between devices, name_the_roads(): item_now = jax.lax.ppermute(item_now, axis_name=chip_axis, perm=items)  76.3 us
    reduce_scatter x1, waiting for transfers between devices, settle(): lax.psum_scatter(grads[4], 'fsdp', scatter_dimension=0, tiled=True)  72.9 us
    reduce_scatter x1, waiting for transfers between devices, settle(): lax.psum_scatter(grads[5], 'fsdp', scatter_dimension=1, tiled=True)  70 us
    reduce_scatter x1, waiting for transfers between devices, settle(): lax.psum_scatter(grads[2], 'fsdp', scatter_dimension=0, tiled=True)  66.3 us
    reduce_scatter x1, waiting for transfers between devices, settle(): lax.psum_scatter(grads[0], 'fsdp', scatter_dimension=0, tiled=True)  66.2 us
    reduce_scatter x1, waiting for transfers between devices, settle(): lax.psum_scatter(grads[1], 'fsdp', scatter_dimension=0, tiled=True)  66.1 us
    psum x1, blocking collectives, local(): lax.psum((gain_one, shift_one, query_kernel_full, key_kernel_full, value_...  41.6 us
  transfers between devices with their start and end apart: 40, of which 27 were waited for; matrix products, arithmetic and copies ran while one was open for 12% of the time, Pallas kernels for 0%

profile of v1, /device:TPU:0, one launch (start us, length us, event | category | flops | bytes accessed | tf_op | source)
XLA Modules:
  0.0 1032.6 jit_solution(2704675430273110538)
XLA Ops:
  16.1 32.3 %all_gather.15 = bf16[192,768]{0,1:T(8,128)(2,1)S(1)} all-gather(bf16[192,96]{0,1:T(8,128)(2,1)S(1)} %copy.43), channel_id=1, replica_groups=mesh['fsdp'=8,'tp'=4] {'fsdp'}, dimensions={1}, use_global_device_ids=true | all-gather | bytes 331776 | tf_op jit(solution)/shard_map/all_gather | solution.py:178
  48.4 33.1 %all_gather.13 = bf16[768,192]{1,0:T(8,128)(2,1)} all-gather(bf16[96,192]{1,0:T(8,128)(2,1)S(1)} %copy-done.117), channel_id=1, replica_groups=mesh['fsdp'=8,'tp'=4] {'fsdp'}, dimensions={0}, use_global_device_ids=true | all-gather | bytes 331776 | tf_op jit(solution)/shard_map/all_gather | solution.py:175
  81.6 31.0 %all_gather.14 = bf16[768,192]{1,0:T(8,128)(2,1)S(1)} all-gather(bf16[96,192]{1,0:T(8,128)(2,1)S(1)} %copy-done.118), channel_id=1, replica_groups=mesh['fsdp'=8,'tp'=4] {'fsdp'}, dimensions={0}, use_global_device_ids=true | all-gather | bytes 331776 | tf_op jit(solution)/shard_map/all_gather | solution.py:176
  116.0 31.8 %all_gather.12 = bf16[768,192]{1,0:T(8,128)(2,1)S(1)} all-gather(bf16[96,192]{1,0:T(8,128)(2,1)} %param.47), channel_id=1, replica_groups=mesh['fsdp'=8,'tp'=4] {'fsdp'}, dimensions={0}, use_global_device_ids=true | all-gather | bytes 331776 | tf_op jit(solution)/shard_map/all_gather | solution.py:177
  165.2 29.2 %reduce-scatter.17.cloned.1.call-done = bf16[256,768]{1,0:T(8,128)(2,1)} async-done(((bf16[1024,768]{1,0:T(8,128)(2,1)}), bf16[256,768]{1,0:T(8,128)(2,1)}) %reduce-scatter.17.cloned.1.call-update) | async-done | bytes 393232 | tf_op jit(solution)/shard_map/reduce_scatter | solution.py:200
  199.1 9.0 collective-permute-done.6
  208.4 7.1 collective-permute-done.8
  232.3 25.7 %reduce-scatter.21.cloned.1.call-done = bf16[256,768]{1,0:T(8,128)(2,1)} async-done(((bf16[1024,768]{1,0:T(8,128)(2,1)}), bf16[256,768]{1,0:T(8,128)(2,1)}) %reduce-scatter.21.cloned.1.call-update) | async-done | bytes 393232 | tf_op jit(solution)/shard_map/reduce_scatter | solution.py:200
  294.3 21.5 %all-gather.5.cloned.1.call-done = bf16[768,768]{0,1:T(8,128)(2,1)} async-done(((bf16[768,96]{0,1:T(8,128)(2,1)}), bf16[768,768]{0,1:T(8,128)(2,1)}) %all-gather.5.cloned.1.call-update) | async-done | bytes 1179664 | tf_op jit(solution)/shard_map/all_gather | solution.py:180
  342.5 14.2 %collective-permute-done.14 = bf16[256,768]{1,0:T(8,128)(2,1)S(1)} collective-permute-done((bf16[256,768]{1,0:T(8,128)(2,1)S(1)}, bf16[256,768]{1,0:T(8,128)(2,1)S(1)}, u32[]{:S(2)}, u32[]{:S(2)}) %collective-permute-start.14) | collective-permute-done | bytes 393248 | tf_op jit(solution)/shard_map/ppermute | solution.py:35
  370.2 26.4 %reduce-scatter.25.cloned.1.call-done = bf16[256,768]{1,0:T(8,128)(2,1)} async-done(((bf16[1024,768]{1,0:T(8,128)(2,1)}), bf16[256,768]{1,0:T(8,128)(2,1)}) %reduce-scatter.25.cloned.1.call-update) | async-done | bytes 393232 | tf_op jit(solution)/shard_map/reduce_scatter | solution.py:200
  403.0 7.0 collective-permute-done.21
  410.0 8.4 collective-permute-done.15
  444.6 6.8 multiply_convert_fusion.4
  467.0 7.6 multiply_convert_fusion.1
  572.2 16.0 %reduce-scatter.27.cloned.1.call-done = bf16[256,768]{1,0:T(8,128)(2,1)} async-done(((bf16[1024,768]{1,0:T(8,128)(2,1)}), bf16[256,768]{1,0:T(8,128)(2,1)}) %reduce-scatter.27.cloned.1.call-update) | async-done | bytes 393232 | tf_op jit(solution)/shard_map/reduce_scatter | solution.py:200
  588.2 30.5 %reduce-scatter.31.cloned.1.call-done = bf16[256,768]{1,0:T(8,128)(2,1)} async-done(((bf16[1024,768]{1,0:T(8,128)(2,1)}), bf16[256,768]{1,0:T(8,128)(2,1)}) %reduce-scatter.31.cloned.1.call-update) | async-done | bytes 393232 | tf_op jit(solution)/shard_map/reduce_scatter | solution.py:200
  622.5 41.6 %all-reduce.28 = (f32[768]{0:T(1024)}, f32[768]{0:T(1024)}, f32[3,768]{1,0:T(4,128)}, f32[3,768]{1,0:T(4,128)}, f32[3,768]{1,0:T(4,128)}, /*index=5*/f32[768]{0:...) all-reduce(f32[768]{0:T(1024)S(1)} %add.646, ...), channel_id=1, replica_groups=mesh['fsdp'=8,'tp'=4] {'fsdp','tp'}, use_global_device_ids=true, to_apply=%region_38.39 | all-reduce | flops 13824 | bytes 110592 | tf_op jit(solution)/shard_map/psum | solution.py:365
  667.4 12.3 %reduce-scatter.19.cloned.1.call-done = bf16[256,768]{1,0:T(8,128)(2,1)} async-done(((bf16[1024,768]{1,0:T(8,128)(2,1)}), bf16[256,768]{1,0:T(8,128)(2,1)}) %reduce-scatter.19.cloned.1.call-update) | async-done | bytes 393232 | tf_op jit(solution)/shard_map/reduce_scatter | solution.py:200
  683.4 70.0 %reduce-scatter.41.cloned.1.call-done = f32[768,96]{0,1:T(8,128)} async-done(((f32[768,768]{0,1:T(8,128)}), f32[768,96]{0,1:T(8,128)}) %reduce-scatter.41.cloned.1.call-update) | async-done | bytes 294928 | tf_op jit(solution)/shard_map/reduce_scatter | solution.py:191
  753.4 72.9 %reduce-scatter.39.cloned.1.call-done = f32[96,768]{1,0:T(8,128)} async-done(((f32[768,768]{1,0:T(8,128)}), f32[96,768]{1,0:T(8,128)}) %reduce-scatter.39.cloned.1.call-update) | async-done | bytes 294928 | tf_op jit(solution)/shard_map/reduce_scatter | solution.py:190
  826.3 66.3 %reduce-scatter.37.cloned.1.call-done = f32[96,192]{1,0:T(8,128)} async-done(((f32[768,192]{1,0:T(8,128)}), f32[96,192]{1,0:T(8,128)}) %reduce-scatter.37.cloned.1.call-update) | async-done | bytes 73744 | tf_op jit(solution)/shard_map/reduce_scatter | solution.py:188
  892.7 66.1 %reduce-scatter.35.cloned.1.call-done = f32[96,192]{1,0:T(8,128)} async-done(((f32[768,192]{1,0:T(8,128)}), f32[96,192]{1,0:T(8,128)}) %reduce-scatter.35.cloned.1.call-update) | async-done | bytes 73744 | tf_op jit(solution)/shard_map/reduce_scatter | solution.py:187
  958.8 66.2 %reduce-scatter.33.cloned.1.call-done = f32[96,192]{1,0:T(8,128)} async-done(((f32[768,192]{1,0:T(8,128)}), f32[96,192]{1,0:T(8,128)}) %reduce-scatter.33.cloned.1.call-update) | async-done | bytes 73744 | tf_op jit(solution)/shard_map/reduce_scatter | solution.py:186
  (644 shorter events, 280.9 us)
Async XLA Ops:
  8.1 186.3 %reduce-scatter.17.cloned.1.call-start = ((), (), s32[]{:S(2)}) async-start(), calls=%async_computation.14 | async-start | bytes 1966080 | tf_op jit(solution)/shard_map/reduce_scatter | solution.py:200
  13.4 101.1 %collective-permute-start = (bf16[256,768]{1,0:T(8,128)(2,1)}, bf16[256,768]{1,0:T(8,128)(2,1)}, u32[]{:S(2)}, u32[]{:S(2)}) collective-permute-start(bf16[256,768]{1,0:T(8,128)(2,1)} %get-tuple-element.215), channel_id=1, source_target_pairs={{0,1},{1,2},{2,3},{3,0},{4,5},{5,6},{6,7},{7,4},{8,9},{9,10},{10,1... | collective-permute-start | bytes 1179656 | tf_op jit(solution)/shard_map/ppermute | solution.py:35
  13.9 135.1 %collective-permute-start.1 = (bf16[256,768]{1,0:T(8,128)(2,1)}, bf16[256,768]{1,0:T(8,128)(2,1)}, u32[]{:S(2)}, u32[]{:S(2)}) collective-permute-start(bf16[256,768]{1,0:T(8,128)(2,1)} %get-tuple-element.215), channel_id=1, source_target_pairs={{0,3},{1,0},{2,1},{3,2},{4,7},{5,4},{6,5},{7,6},{8,11},{9,8},{10,9... | collective-permute-start | bytes 1179656 | tf_op jit(solution)/shard_map/ppermute | solution.py:45
  114.4 35.6 %collective-permute-start.2 = (bf16[256,768]{1,0:T(8,128)(2,1)}, bf16[256,768]{1,0:T(8,128)(2,1)}, u32[]{:S(2)}, u32[]{:S(2)}) collective-permute-start(bf16[256,768]{1,0:T(8,128)(2,1)} %collective-permute-done), channel_id=1, source_target_pairs={{0,1},{1,2},{2,3},{3,0},{4,5},{5,6},{6,7},{7,4},{8,9},{9,10},{10,1... | collective-permute-start | bytes 1179656 | tf_op jit(solution)/shard_map/ppermute | solution.py:35
  165.1 93.0 %reduce-scatter.21.cloned.1.call-start = ((), (), s32[]{:S(2)}) async-start(), calls=%async_computation.18 | async-start | bytes 1966080 | tf_op jit(solution)/shard_map/reduce_scatter | solution.py:200
  230.2 59.4 %all-gather.3.cloned.1.call-start = ((), (), s32[]{:S(2)}) async-start(), calls=%async_computation.15 | async-start | bytes 1327104 | tf_op jit(solution)/shard_map/all_gather | solution.py:179
  230.8 85.1 %all-gather.5.cloned.1.call-start = ((), (), s32[]{:S(2)}) async-start(), calls=%async_computation.16 | async-start | bytes 1327104 | tf_op jit(solution)/shard_map/all_gather | solution.py:180
  231.7 35.9 %collective-permute-start.18 = (bf16[256,768]{1,0:T(8,128)(2,1)}, bf16[256,768]{1,0:T(8,128)(2,1)}, u32[]{:S(2)}, u32[]{:S(2)}) collective-permute-start(bf16[256,768]{1,0:T(8,128)(2,1)} %get-tuple-element.220), channel_id=1, source_target_pairs={{0,1},{1,2},{2,3},{3,0},{4,5},{5,6},{6,7},{7,4},{8,9},{9,10},{10,1... | collective-permute-start | bytes 1179656 | tf_op jit(solution)/shard_map/ppermute | solution.py:35
  231.8 138.4 %reduce-scatter.29.cloned.1.call-start = ((), (), s32[]{:S(2)}) async-start(), calls=%async_computation.22 | async-start | bytes 1966080 | tf_op jit(solution)/shard_map/reduce_scatter | solution.py:200
  324.5 72.1 %reduce-scatter.25.cloned.1.call-start = ((), (), s32[]{:S(2)}) async-start(), calls=%async_computation.20 | async-start | bytes 1966080 | tf_op jit(solution)/shard_map/reduce_scatter | solution.py:200
  332.5 24.2 %collective-permute-start.14 = (bf16[256,768]{1,0:T(8,128)(2,1)S(1)}, bf16[256,768]{1,0:T(8,128)(2,1)S(1)}, u32[]{:S(2)}, u32[]{:S(2)}) collective-permute-start(bf16[256,768]{1,0:T(8,128)(2,1)S(1)} %collective-permute-done.12), channel_id=1, source_target_pairs={{0,1},{1,2},{2,3},{3,0},{4,5},{5,6},{6,7},{7,4},{8,9},{9,10},{10,1... | collective-permute-start | bytes 1179656 | tf_op jit(solution)/shard_map/ppermute | solution.py:35
  332.8 24.1 %collective-permute-start.4 = (bf16[256,768]{1,0:T(8,128)(2,1)S(1)}, bf16[256,768]{1,0:T(8,128)(2,1)S(1)}, u32[]{:S(2)}, u32[]{:S(2)}) collective-permute-start(bf16[256,768]{1,0:T(8,128)(2,1)S(1)} %get-tuple-element.209), channel_id=1, source_target_pairs={{0,3},{1,0},{2,1},{3,2},{4,7},{5,4},{6,5},{7,6},{8,11},{9,8},{10,9... | collective-permute-start | bytes 1179656 | tf_op jit(solution)/shard_map/ppermute | solution.py:45
  341.0 20.6 %collective-permute-start.5 = (bf16[256,768]{1,0:T(8,128)(2,1)S(1)}, bf16[256,768]{1,0:T(8,128)(2,1)S(1)}, u32[]{:S(2)}, u32[]{:S(2)}) collective-permute-start(bf16[256,768]{1,0:T(8,128)(2,1)S(1)} %collective-permute-done.3), channel_id=1, source_target_pairs={{0,1},{1,2},{2,3},{3,0},{4,5},{5,6},{6,7},{7,4},{8,9},{9,10},{10,1... | collective-permute-start | bytes 1179656 | tf_op jit(solution)/shard_map/ppermute | solution.py:35
  370.1 200.4 %reduce-scatter.43.cloned.1.call-start = ((), (), s32[]{:S(2)}) async-start(), calls=%async_computation.29 | async-start | bytes 884736
  402.8 17.9 %collective-permute-start.16 = (bf16[256,768]{1,0:T(8,128)(2,1)S(1)}, bf16[256,768]{1,0:T(8,128)(2,1)S(1)}, u32[]{:S(2)}, u32[]{:S(2)}) collective-permute-start(bf16[256,768]{1,0:T(8,128)(2,1)S(1)} %get-tuple-element.205), channel_id=1, source_target_pairs={{0,3},{1,0},{2,1},{3,2},{4,7},{5,4},{6,5},{7,6},{8,11},{9,8},{10,9... | collective-permute-start | bytes 1179656 | tf_op jit(solution)/shard_map/ppermute | solution.py:45
  495.1 93.1 %reduce-scatter.27.cloned.1.call-start = ((), (), s32[]{:S(2)}) async-start(), calls=%async_computation.21 | async-start | bytes 1966080 | tf_op jit(solution)/shard_map/reduce_scatter | solution.py:200
  506.4 112.3 %reduce-scatter.31.cloned.1.call-start = ((), (), s32[]{:S(2)}) async-start(), calls=%async_computation.23 | async-start | bytes 1966080 | tf_op jit(solution)/shard_map/reduce_scatter | solution.py:200
  511.8 152.8 %reduce-scatter.23.cloned.1.call-start = ((), (), s32[]{:S(2)}) async-start(), calls=%async_computation.19 | async-start | bytes 1966080 | tf_op jit(solution)/shard_map/reduce_scatter | solution.py:200
  516.8 162.9 %reduce-scatter.19.cloned.1.call-start = ((), (), s32[]{:S(2)}) async-start(), calls=%async_computation.17 | async-start | bytes 1966080 | tf_op jit(solution)/shard_map/reduce_scatter | solution.py:200
  521.4 232.0 %reduce-scatter.41.cloned.1.call-start = ((), (), s32[]{:S(2)}) async-start(), calls=%async_computation.28 | async-start | bytes 2654208 | tf_op jit(solution)/shard_map/reduce_scatter | solution.py:191
  528.6 297.8 %reduce-scatter.39.cloned.1.call-start = ((), (), s32[]{:S(2)}) async-start(), calls=%async_computation.27 | async-start | bytes 2654208 | tf_op jit(solution)/shard_map/reduce_scatter | solution.py:190
  535.4 357.3 %reduce-scatter.37.cloned.1.call-start = ((), (), s32[]{:S(2)}) async-start(), calls=%async_computation.26 | async-start | bytes 884736 | tf_op jit(solution)/shard_map/reduce_scatter | solution.py:188
  546.1 412.6 %reduce-scatter.35.cloned.1.call-start = ((), (), s32[]{:S(2)}) async-start(), calls=%async_computation.25 | async-start | bytes 884736 | tf_op jit(solution)/shard_map/reduce_scatter | solution.py:187
  558.3 466.7 %reduce-scatter.33.cloned.1.call-start = ((), (), s32[]{:S(2)}) async-start(), calls=%async_computation.24 | async-start | bytes 884736 | tf_op jit(solution)/shard_map/reduce_scatter | solution.py:186
  (196 other events, 2304.3 us)
Sparse Core Ops, SparseCore 0:
  165.2 29.0 reduce-scatter.16
  230.3 27.7 reduce-scatter.20
  324.7 34.0 reduce-scatter.28
  370.2 26.3 reduce-scatter.24
Sparse Core Ops, SparseCore 1:
  232.8 41.2 all-gather.2
  276.1 39.6 all-gather.4
  495.2 63.3 reduce-scatter.42
  561.2 27.0 reduce-scatter.26
  590.8 27.9 reduce-scatter.30
  621.3 27.9 reduce-scatter.22
  651.7 27.9 reduce-scatter.18
  683.6 69.7 reduce-scatter.40
  757.4 68.9 reduce-scatter.38
  830.2 62.4 reduce-scatter.36
  896.4 62.3 reduce-scatter.34
  962.7 62.3 reduce-scatter.32
